TPU v7x, 32 devices: a whole 2x2x4 slice. The times are simulated.
32 devices in a mesh: row: 8 (over z, y), col: 4 (over x, core).
Axes of the slice: x: 2, y: 2, z: 4, core: 2. Of those that a mesh axis runs over, the one named last changes fastest.
Arguments:
- spectra: bfloat16 [1024, 16, 128], P(('row', 'col')), may hold values from -4 to 4
- window_flags: int32 [1024, 64], P(('row', 'col')), may hold values 0 or 1
- pair_mask: int32 [1024, 1024], P('row', 'col'), may hold values 0 or 1
- misfit_weight: bfloat16 [16, 1024, 1024], P(None, 'row', 'col'), may hold values from 0.0099487305 to 0.099609375
- observed: bfloat16 [2, 16, 1024, 1024], P(None, None, 'row', 'col'), may hold values from -6 to 6
Outputs:
- grad_first: bfloat16 [1024, 16, 128], P(('row', 'col'))
- grad_second: bfloat16 [4, 256, 16, 128], P('col', 'row')
All inputs are finite; a program needn't handle non-finite values. No bound on the sum of `window_flags` or of `pair_mask` on one device may be relied on, other than what follows from the above.
Results may differ from a plain program's by a relative error of at most 0.019.
Values may be sent and summed in bfloat16 or wider, within the bound.
A program may use at most 64 MiB of HBM per device.

v0:
```python
import functools

import jax
import jax.numpy as jnp
from jax import lax
from jax.experimental import pallas as pl
from jax.experimental.pallas import tpu as pltpu
from jax.sharding import PartitionSpec as P

MESH = pl.DeviceIdType.MESH
GROUP = 2
LAG_Y, LAG_B, LAG_C = 3, 3, 7


def kernel(
    n_row, n_col, chunks, group,
    raw_hbm, flags_hbm, mask_hbm, w_hbm, obs_hbm, out_first, out_second,
    raw, flags, mask, own,
    v1, v2, w_v, obs_v, gf, gf_sum, rc, rx, sums, halves, last, ry,
    in_sem, own_sem, fs, fr, zs, zr, lz, ys, yr,
    cs, cr, ps, pr, hs, hr, bs, br,
):
    ratio = n_row // n_col
    n_z = n_row // ratio
    n_x = n_col // 2
    bits = n_z.bit_length() - 1
    row, col = lax.axis_index("row"), lax.axis_index("col")
    z, y = row // ratio, row % ratio
    x, core = col // 2, col % 2
    shard = own.shape[1]
    first_rows = n_col * shard
    second_rows = ratio * first_rows
    half = own.shape[2] // 2

    def col_at(step):
        return ((x + step) % n_x) * 2 + core

    partner = x * 2 + (1 - core)

    def row_y(step):
        return z * ratio + (y + step) % ratio

    def row_z(step):
        return ((z + step) % n_z) * ratio + y

    def span(k):
        return pl.ds(k * group, group)

    def remote(src, dst, ssem, rsem, to_row, to_col):
        return pltpu.make_async_remote_copy(
            src_ref=src, dst_ref=dst, send_sem=ssem, recv_sem=rsem,
            device_id=(to_row, to_col), device_id_type=MESH,
        )

    def send_f(k, d):
        return remote(own.at[span(k)], v1.at[span(k), col], fs.at[d - 1], fr.at[k], row, (col + d) % n_col)

    def send_z(k, d):
        return remote(own.at[span(k)], v2.at[span(k), y, col], zs.at[d - 1], zr.at[k], row_z(d), z)

    def send_y(k, d, src):
        return remote(src, v2.at[span(k), y], ys.at[d - 1], yr.at[d - 1, k], row_y(d), col)

    def send_c(k):
        return remote(gf.at[span(k), :, 1 - core], rc.at[span(k)], cs, cr.at[k], row, partner)

    def send_p(k, d):
        return remote(gf_sum.at[span(k), (x + d) % n_x], rx.at[d - 1, span(k)], ps.at[d - 1], pr.at[d - 1, k], row, col_at(d))

    def bit(b):
        return (z // 2**b) % 2

    def row_bit(b):
        return (z + (1 - 2 * bit(b)) * 2**b) * ratio + y

    def send_b(k, b):
        return remote(sums[b].at[span(k), :, 1 - bit(b)], halves[b].at[span(k)], bs.at[b], br.at[b, k], row_bit(b), col)

    def send_h(k, d):
        return remote(last.at[span(k), (y + d) % ratio], ry.at[d - 1, span(k)], hs.at[d - 1], hr.at[d - 1, k], row_y(d), col)

    home = z == col

    load_w = pltpu.make_async_copy(w_hbm, w_v, in_sem.at[0])
    load_obs = pltpu.make_async_copy(obs_hbm, obs_v, in_sem.at[1])
    load_own = pltpu.make_async_copy(own, v1.at[:, col], own_sem)
    load_raw = pltpu.make_async_copy(raw_hbm, raw, in_sem.at[2])
    load_flags = pltpu.make_async_copy(flags_hbm, flags, in_sem.at[3])
    load_mask = pltpu.make_async_copy(mask_hbm, mask, in_sem.at[4])
    load_raw.start()
    load_flags.start()

    barrier = pltpu.get_barrier_semaphore()

    def tell(to_row, to_col):
        pl.semaphore_signal(barrier, inc=1, device_id=(to_row, to_col), device_id_type=MESH)

    @pl.when(jnp.logical_not(home))
    def _():
        for j in range(n_col):
            tell(col * ratio + y, j)

    for b in range(bits):
        tell(row_bit(b), col)
    for d in range(1, ratio):
        tell(row_y(d), col)
    for d in range(1, n_col):
        tell(row, (col + d) % n_col)

    load_raw.wait()
    load_flags.wait()
    load_mask.start()
    load_w.start()
    load_obs.start()
    flag_value = flags[...].astype(jnp.float32)
    flag_both = jnp.concatenate([flag_value, flag_value], axis=1)
    flagged = raw[...].astype(jnp.float32) * flag_both[:, None, :]
    own[...] = jnp.transpose(flagged, (1, 0, 2)).astype(jnp.bfloat16)
    load_own.start()
    pl.semaphore_wait(barrier, n_col - 1 + n_z - 1 + bits + ratio - 1)

    @pl.loop(0, chunks)
    def _(k):
        for d in range(n_z - 1, 0, -1):
            send_z(k, d).start()
        for d in range(1, n_col):
            send_f(k, d).start()

    load_own.wait()

    def wait_first(k):
        got = v1.at[span(k), pl.ds(0, n_col - 1)]
        pltpu.make_async_copy(got, got, fr.at[k]).wait()

    def local_copy(k):
        return pltpu.make_async_copy(v1.at[span(k)], v2.at[span(k), y], lz.at[k])

    lane = lax.broadcasted_iota(jnp.int32, (1, 2 * half), 1)
    low_plus = jnp.where(lane < half, 1.0, -1.0).astype(jnp.float32)

    def compute(f):
        a = v1[f].astype(jnp.float32).reshape(first_rows, 2 * half)
        b = v2[f].astype(jnp.float32).reshape(second_rows, 2 * half).astype(jnp.bfloat16)
        turned = pltpu.roll(a, half, 1) * low_plus
        w = jnp.concatenate([a, turned], axis=0).astype(jnp.bfloat16)
        cross = lax.dot_general(w, b, (((1,), (1,)), ((), ())), preferred_element_type=jnp.float32)
        scale = mask[...].astype(jnp.float32) * w_v[f].astype(jnp.float32)
        res = jnp.concatenate(
            [
                (scale * (cross[:first_rows] - obs_v[0, f].astype(jnp.float32))).astype(jnp.bfloat16),
                (scale * (cross[first_rows:] - obs_v[1, f].astype(jnp.float32))).astype(jnp.bfloat16),
            ],
            axis=0,
        )
        t = jnp.dot(res, b, preferred_element_type=jnp.float32)
        g1 = t[:first_rows] - pltpu.roll(t[first_rows:], half, 1) * low_plus
        gf[f] = g1.reshape(n_x, 2, shard, 2 * half).astype(jnp.bfloat16)
        g2 = lax.dot_general(res, w, (((0,), (0,)), ((), ())), preferred_element_type=jnp.float32)
        sums[0][f] = g2.reshape(n_z // 2, 2, ratio, shard, 2 * half).astype(jnp.bfloat16)

    lag_y, lag_c = LAG_Y, LAG_C
    lag_b = [lag_y + LAG_B * (b + 1) for b in range(bits)]

    @pl.loop(0, chunks + max(lag_b[-1], lag_c))
    def _(it):
        @pl.when(it < chunks)
        def _():
            @pl.when(home)
            def _():
                wait_first(it)
                for d in range(1, ratio):
                    send_y(it, d, v1.at[span(it)]).start()
                local_copy(it).start()

            @pl.when(jnp.logical_not(home))
            def _():
                got = v2.at[span(it), y]
                pltpu.make_async_copy(got, got, zr.at[it]).wait()
                for d in range(1, ratio):
                    send_y(it, d, v2.at[span(it), y]).start()

        @pl.when(jnp.logical_and(it >= lag_y, it < chunks + lag_y))
        def _():
            k = it - lag_y

            @pl.when(k == 0)
            def _():
                load_mask.wait()
                load_w.wait()
                load_obs.wait()

            for d in range(1, ratio):
                send_y(k, d, v2.at[span(k), y]).wait_recv()

            @pl.when(home)
            def _():
                local_copy(k).wait()

            @pl.when(jnp.logical_not(home))
            def _():
                wait_first(k)

            for i in range(group):
                compute(k * group + i)
            send_c(k).start()
            send_b(k, 0).start()

        for b in range(bits):
            @pl.when(jnp.logical_and(it >= lag_b[b], it < chunks + lag_b[b]))
            def _():
                k = it - lag_b[b]
                send_b(k, b).wait_recv()
                total = sums[b][span(k), :, bit(b)].astype(jnp.float32) + halves[b][span(k)].astype(jnp.float32)
                if b + 1 < bits:
                    sums[b + 1][span(k)] = total.reshape(
                        group, n_z // 2 ** (b + 2), 2, ratio, shard, 2 * half
                    ).astype(jnp.bfloat16)
                    send_b(k, b + 1).start()
                else:
                    last[span(k)] = total[:, 0].astype(jnp.bfloat16)
                    for d in range(1, ratio):
                        send_h(k, d).start()

        @pl.when(jnp.logical_and(it >= lag_c, it < chunks + lag_c))
        def _():
            k = it - lag_c
            send_c(k).wait_recv()
            total = gf[span(k), :, core].astype(jnp.float32) + rc[span(k)].astype(jnp.float32)
            gf_sum[span(k)] = total.astype(jnp.bfloat16)
            for d in range(1, n_x):
                send_p(k, d).start()

    @pl.loop(0, chunks)
    def _(k):
        for d in range(1, n_x):
            send_p(k, d).wait_recv()
        total = gf_sum[span(k), x].astype(jnp.float32)
        for d in range(1, n_x):
            total = total + rx[d - 1, span(k)].astype(jnp.float32)
        out_first[span(k)] = total.astype(jnp.bfloat16)
        total = last[span(k), y].astype(jnp.float32)
        for d in range(1, ratio):
            send_h(k, d).wait_recv()
            total = total + ry[d - 1, span(k)].astype(jnp.float32)
        out_second[span(k)] = total.astype(jnp.bfloat16)

    def sent(ref, sem):
        pltpu.make_async_copy(ref, ref, sem).wait()

    for d in range(1, n_col):
        sent(own, fs.at[d - 1])
    for d in range(1, n_z):
        sent(own, zs.at[d - 1])
    for d in range(1, ratio):
        sent(v1, ys.at[d - 1])
        sent(own, hs.at[d - 1])
    for d in range(1, n_x):
        sent(own, ps.at[d - 1])
    sent(rc, cs)
    for b in range(bits):
        sent(halves[b], bs.at[b])


def turn_kernel(first, second, out_first, out_second):
    for src, dst in ((first, out_first), (second, out_second)):
        dst[...] = jnp.transpose(src[...].astype(jnp.float32), (1, 0, 2)).astype(jnp.bfloat16)


def per_device(n_row, n_col, spectra, window_flags, pair_mask, misfit_weight, observed):
    shard, freqs, width = spectra.shape
    ratio = n_row // n_col
    n_z, n_x = n_row // ratio, n_col // 2
    bits = n_z.bit_length() - 1
    group = GROUP if freqs % GROUP == 0 else 1
    chunks = freqs // group
    bf = jnp.bfloat16
    vm = lambda *shape: pltpu.VMEM(shape, bf)
    dma = lambda *shape: pltpu.SemaphoreType.DMA(shape)
    first, second = pl.pallas_call(
        functools.partial(kernel, n_row, n_col, chunks, group),
        out_shape=[jax.ShapeDtypeStruct((freqs, shard, width), bf)] * 2,
        in_specs=[
            pl.BlockSpec(memory_space=pl.ANY),
        ] * 5,
        out_specs=[pl.BlockSpec(memory_space=pltpu.VMEM)] * 2,
        scratch_shapes=[
            pltpu.VMEM(spectra.shape, bf),
            pltpu.VMEM(window_flags.shape, window_flags.dtype),
            pltpu.VMEM(pair_mask.shape, pair_mask.dtype),
            vm(freqs, shard, width),
            vm(freqs, n_col, shard, width),
            vm(freqs, ratio, n_col, shard, width),
            pltpu.VMEM(misfit_weight.shape, bf),
            pltpu.VMEM(observed.shape, bf),
            vm(freqs, n_x, 2, shard, width),
            vm(freqs, n_x, shard, width),
            vm(freqs, n_x, shard, width),
            vm(n_x - 1, freqs, shard, width),
            [vm(freqs, n_z // 2 ** (b + 1), 2, ratio, shard, width) for b in range(bits)],
            [vm(freqs, n_z // 2 ** (b + 1), ratio, shard, width) for b in range(bits)],
            vm(freqs, ratio, shard, width),
            vm(ratio - 1, freqs, shard, width),
            dma(5), pltpu.SemaphoreType.DMA,
            dma(n_col - 1), dma(chunks),
            dma(n_z - 1), dma(chunks), dma(chunks),
            dma(ratio - 1), dma(ratio - 1, chunks),
            pltpu.SemaphoreType.DMA, dma(chunks),
            dma(n_x - 1), dma(n_x - 1, chunks),
            dma(ratio - 1), dma(ratio - 1, chunks),
            dma(bits), dma(bits, chunks),
        ],
        compiler_params=pltpu.CompilerParams(collective_id=0, has_side_effects=True),
        name="adjoint",
    )(spectra, window_flags, pair_mask, misfit_weight, observed)
    parts = 2 if shard % 32 == 0 else 1
    first, second = pl.pallas_call(
        turn_kernel,
        out_shape=[jax.ShapeDtypeStruct((shard, freqs, width), bf)] * 2,
        grid=(parts,),
        in_specs=[pl.BlockSpec((freqs, shard // parts, width), lambda i: (0, i, 0))] * 2,
        out_specs=[pl.BlockSpec((shard // parts, freqs, width), lambda i: (i, 0, 0))] * 2,
        name="turn",
    )(first, second)
    return first, second[None]


def solution(mesh):
    placed = (
        P(("row", "col"), None, None),
        P(("row", "col"), None),
        P("row", "col"),
        P(None, "row", "col"),
        P(None, None, "row", "col"),
    )
    return jax.shard_map(
        functools.partial(per_device, mesh.shape["row"], mesh.shape["col"]),
        mesh=mesh,
        in_specs=placed,
        out_specs=(P(("row", "col"), None, None), P("col", "row", None, None)),
        check_vma=False,
    )
```

profile of v0, /device:TPU:0, one launch (start us, length us, event | category | flops | bytes accessed | tf_op | source)
XLA Modules:
  0.0 40.4 jit_solution(17316857738869250074)
XLA Ops:
  0.6 38.1 %adjoint.1 = (bf16[16,32,128]{2,1,0:T(8,128)(2,1)}, bf16[16,32,128]{2,1,0:T(8,128)(2,1)}) custom-call(bf16[32,16,128]{2,1,0:T(8,128)(2,1)} %raw_hbm.1, s32[32,64]{1,0:T(8,128)} %flags_hbm.1, s32[128,256]{1,0:T(8,128)} %mask_hbm.1, bf16[16,128,256]{2,1,0:T(8,128)(2,1)} %w_hbm.1, bf16[2,16,128,256]{3,2,1,0:T(8,128)(2,1)} %obs_hbm.1), custom_call_target="tpu_custom_call" | custom-call | tf_op jit(solution)/shard_map/adjoint/pallas_call | solution.py:279
  38.7 1.7 %turn.1 = (bf16[32,16,128]{2,1,0:T(8,128)(2,1)}, bf16[32,16,128]{2,1,0:T(8,128)(2,1)}) custom-call(bf16[16,32,128]{2,1,0:T(8,128)(2,1)} %get-tuple-element.6.first, bf16[16,32,128]{2,1,0:T(8,128)(2,1)} %get-tuple-element.7.second), custom_call_target="tpu_custom_call" | custom-call | tf_op jit(solution)/shard_map/turn/pallas_call | solution.py:316
where the time goes:
time: 40.6 us; the launch traced here: 40.4 us
  Pallas kernels  39.7 us (98%)
  between operations  0.64 us (2%)
    pallas_call x1, Pallas kernels, per_device(): pl.pallas_call(functools.partial(kernel, n_row, n_col, chunks, group), ou...  38.1 us
    pallas_call x1, Pallas kernels, per_device(): pl.pallas_call(turn_kernel, out_shape=[jax.ShapeDtypeStruct((shard, freqs...  1.66 us

commit v1 on v0

--- a/solution.py
+++ b/solution.py
@@ -9,16 +9,27 @@
 
 MESH = pl.DeviceIdType.MESH
 GROUP = 2
-LAG_Y, LAG_B, LAG_C = 3, 3, 7
+LAG_Y = 3
+LAG_STAGES = (4, 4, 4)
+LAG_C, LAG_P = 3, 4
+Z_FIRST_FROM, Z_FIRST_TO = 0, 8
+
+
+def z_first(k, chunks):
+    return jnp.logical_and(k * 16 >= Z_FIRST_FROM * chunks, k * 16 < Z_FIRST_TO * chunks)
+
+
+def z_first_count(chunks):
+    return sum(Z_FIRST_FROM * chunks <= k * 16 < Z_FIRST_TO * chunks for k in range(chunks))
 
 
 def kernel(
     n_row, n_col, chunks, group,
     raw_hbm, flags_hbm, mask_hbm, w_hbm, obs_hbm, out_first, out_second,
     raw, flags, mask, own,
-    v1, v2, w_v, obs_v, gf, gf_sum, rc, rx, sums, halves, last, ry,
-    in_sem, own_sem, fs, fr, zs, zr, lz, ys, yr,
-    cs, cr, ps, pr, hs, hr, bs, br,
+    v1, v2, w_v, obs_v, gf, gf_sum, rc, rx, sums, halves, last, ry, turn_in, thin, thin_in,
+    in_sem, own_sem, fs, fr, zs, zr, lz, hy, ys, yr,
+    cs, cr, ps, pr, hs, hr, bs, br, us, ur, ts, tr,
 ):
     ratio = n_row // n_col
     n_z = n_row // ratio
@@ -58,8 +69,12 @@
     def send_z(k, d):
         return remote(own.at[span(k)], v2.at[span(k), y, col], zs.at[d - 1], zr.at[k], row_z(d), z)
 
-    def send_y(k, d, src):
-        return remote(src, v2.at[span(k), y], ys.at[d - 1], yr.at[d - 1, k], row_y(d), col)
+    def send_home(k, d):
+        return remote(own.at[span(k)], v2.at[span(k), y, col], hy.at[d - 1], yr.at[d - 1, k], row_y(d), z)
+
+    def send_y(k, d):
+        src = v2.at[span(k), y]
+        return remote(src, src, ys.at[d - 1], yr.at[d - 1, k], row_y(d), col)
 
     def send_c(k):
         return remote(gf.at[span(k), :, 1 - core], rc.at[span(k)], cs, cr.at[k], row, partner)
@@ -78,6 +93,12 @@
 
     def send_h(k, d):
         return remote(last.at[span(k), (y + d) % ratio], ry.at[d - 1, span(k)], hs.at[d - 1], hr.at[d - 1, k], row_y(d), col)
+
+    def send_u(k, d):
+        return remote(sums[0].at[span(k), :, :, (y + d) % ratio], turn_in.at[d - 1, span(k)], us.at[d - 1], ur.at[d - 1, k], row_y(d), col)
+
+    def send_t(k, b):
+        return remote(thin[b].at[span(k), :, 1 - bit(b)], thin_in[b].at[span(k)], ts.at[b], tr.at[b, k], row_bit(b), col)
 
     home = z == col
 
@@ -99,6 +120,12 @@
     def _():
         for j in range(n_col):
             tell(col * ratio + y, j)
+
+    @pl.when(home)
+    def _():
+        for d in range(1, ratio):
+            for j in range(n_col):
+                tell(row_y(d), j)
 
     for b in range(bits):
         tell(row_bit(b), col)
@@ -117,7 +144,7 @@
     flagged = raw[...].astype(jnp.float32) * flag_both[:, None, :]
     own[...] = jnp.transpose(flagged, (1, 0, 2)).astype(jnp.bfloat16)
     load_own.start()
-    pl.semaphore_wait(barrier, n_col - 1 + n_z - 1 + bits + ratio - 1)
+    pl.semaphore_wait(barrier, n_col - 1 + n_z - 1 + bits + 2 * (ratio - 1))
 
     @pl.loop(0, chunks)
     def _(k):
@@ -125,6 +152,8 @@
             send_z(k, d).start()
         for d in range(1, n_col):
             send_f(k, d).start()
+        for d in range(1, ratio):
+            send_home(k, d).start()
 
     load_own.wait()
 
@@ -158,107 +187,159 @@
         g2 = lax.dot_general(res, w, (((0,), (0,)), ((), ())), preferred_element_type=jnp.float32)
         sums[0][f] = g2.reshape(n_z // 2, 2, ratio, shard, 2 * half).astype(jnp.bfloat16)
 
-    lag_y, lag_c = LAG_Y, LAG_C
-    lag_b = [lag_y + LAG_B * (b + 1) for b in range(bits)]
-
-    @pl.loop(0, chunks + max(lag_b[-1], lag_c))
-    def _(it):
-        @pl.when(it < chunks)
-        def _():
-            @pl.when(home)
-            def _():
-                wait_first(it)
-                for d in range(1, ratio):
-                    send_y(it, d, v1.at[span(it)]).start()
-                local_copy(it).start()
-
-            @pl.when(jnp.logical_not(home))
-            def _():
-                got = v2.at[span(it), y]
-                pltpu.make_async_copy(got, got, zr.at[it]).wait()
-                for d in range(1, ratio):
-                    send_y(it, d, v2.at[span(it), y]).start()
-
-        @pl.when(jnp.logical_and(it >= lag_y, it < chunks + lag_y))
-        def _():
-            k = it - lag_y
-
-            @pl.when(k == 0)
-            def _():
-                load_mask.wait()
-                load_w.wait()
-                load_obs.wait()
-
-            for d in range(1, ratio):
-                send_y(k, d, v2.at[span(k), y]).wait_recv()
-
-            @pl.when(home)
-            def _():
-                local_copy(k).wait()
-
-            @pl.when(jnp.logical_not(home))
-            def _():
-                wait_first(k)
-
-            for i in range(group):
-                compute(k * group + i)
-            send_c(k).start()
-            send_b(k, 0).start()
-
-        for b in range(bits):
-            @pl.when(jnp.logical_and(it >= lag_b[b], it < chunks + lag_b[b]))
-            def _():
-                k = it - lag_b[b]
-                send_b(k, b).wait_recv()
-                total = sums[b][span(k), :, bit(b)].astype(jnp.float32) + halves[b][span(k)].astype(jnp.float32)
-                if b + 1 < bits:
-                    sums[b + 1][span(k)] = total.reshape(
-                        group, n_z // 2 ** (b + 2), 2, ratio, shard, 2 * half
+    def wide(ref, *at):
+        return ref[at].astype(jnp.float32)
+
+    def second_stage(k, step):
+        if step < bits:
+            @pl.when(z_first(k, chunks))
+            def _():
+                send_b(k, step).wait_recv()
+                total = wide(sums[step], span(k), slice(None), bit(step)) + wide(halves[step], span(k))
+                if step + 1 < bits:
+                    sums[step + 1][span(k)] = total.reshape(
+                        group, n_z // 2 ** (step + 2), 2, ratio, shard, 2 * half
                     ).astype(jnp.bfloat16)
-                    send_b(k, b + 1).start()
+                    send_b(k, step + 1).start()
                 else:
                     last[span(k)] = total[:, 0].astype(jnp.bfloat16)
                     for d in range(1, ratio):
                         send_h(k, d).start()
+        else:
+            @pl.when(z_first(k, chunks))
+            def _():
+                total = wide(last, span(k), y)
+                for d in range(1, ratio):
+                    send_h(k, d).wait_recv()
+                    total = total + wide(ry, d - 1, span(k))
+                out_second[span(k)] = total.astype(jnp.bfloat16)
+
+        @pl.when(jnp.logical_not(z_first(k, chunks)))
+        def _():
+            if step == 0:
+                total = wide(sums[0], span(k), slice(None), slice(None), y)
+                for d in range(1, ratio):
+                    send_u(k, d).wait_recv()
+                    total = total + wide(turn_in, d - 1, span(k))
+            else:
+                b = step - 1
+                send_t(k, b).wait_recv()
+                total = wide(thin[b], span(k), slice(None), bit(b)) + wide(thin_in[b], span(k))
+            if step < bits:
+                thin[step][span(k)] = total.reshape(
+                    group, n_z // 2 ** (step + 1), 2, shard, 2 * half
+                ).astype(jnp.bfloat16)
+                send_t(k, step).start()
+            else:
+                out_second[span(k)] = total[:, 0].astype(jnp.bfloat16)
+
+    lag_y = LAG_Y
+    lag_c = lag_y + LAG_C
+    lag_p = lag_c + LAG_P
+    lag_s, at = [], lag_y
+    for step in range(bits + 1):
+        at = at + LAG_STAGES[min(step, len(LAG_STAGES) - 1)]
+        lag_s.append(at)
+
+    @pl.loop(0, chunks + max(lag_s[-1], lag_p))
+    def _(it):
+        @pl.when(it < chunks)
+        def _():
+            @pl.when(home)
+            def _():
+                wait_first(it)
+                local_copy(it).start()
+
+            @pl.when(jnp.logical_not(home))
+            def _():
+                got = v2.at[span(it), y]
+                pltpu.make_async_copy(got, got, zr.at[it]).wait()
+                for d in range(1, ratio):
+                    send_y(it, d).start()
+
+        @pl.when(jnp.logical_and(it >= lag_y, it < chunks + lag_y))
+        def _():
+            k = it - lag_y
+
+            @pl.when(k == 0)
+            def _():
+                load_mask.wait()
+                load_w.wait()
+                load_obs.wait()
+
+            for d in range(1, ratio):
+                send_y(k, d).wait_recv()
+
+            @pl.when(home)
+            def _():
+                local_copy(k).wait()
+
+            @pl.when(jnp.logical_not(home))
+            def _():
+                wait_first(k)
+
+            for i in range(group):
+                compute(k * group + i)
+
+            @pl.when(z_first(k, chunks))
+            def _():
+                send_b(k, 0).start()
+
+            @pl.when(jnp.logical_not(z_first(k, chunks)))
+            def _():
+                for d in range(1, ratio):
+                    send_u(k, d).start()
+
+            send_c(k).start()
+
+        for step in range(bits + 1):
+            @pl.when(jnp.logical_and(it >= lag_s[step], it < chunks + lag_s[step]))
+            def _():
+                second_stage(it - lag_s[step], step)
 
         @pl.when(jnp.logical_and(it >= lag_c, it < chunks + lag_c))
         def _():
             k = it - lag_c
             send_c(k).wait_recv()
-            total = gf[span(k), :, core].astype(jnp.float32) + rc[span(k)].astype(jnp.float32)
+            total = wide(gf, span(k), slice(None), core) + wide(rc, span(k))
             gf_sum[span(k)] = total.astype(jnp.bfloat16)
             for d in range(1, n_x):
                 send_p(k, d).start()
 
-    @pl.loop(0, chunks)
-    def _(k):
-        for d in range(1, n_x):
-            send_p(k, d).wait_recv()
-        total = gf_sum[span(k), x].astype(jnp.float32)
-        for d in range(1, n_x):
-            total = total + rx[d - 1, span(k)].astype(jnp.float32)
-        out_first[span(k)] = total.astype(jnp.bfloat16)
-        total = last[span(k), y].astype(jnp.float32)
-        for d in range(1, ratio):
-            send_h(k, d).wait_recv()
-            total = total + ry[d - 1, span(k)].astype(jnp.float32)
-        out_second[span(k)] = total.astype(jnp.bfloat16)
-
-    def sent(ref, sem):
-        pltpu.make_async_copy(ref, ref, sem).wait()
-
+        @pl.when(jnp.logical_and(it >= lag_p, it < chunks + lag_p))
+        def _():
+            k = it - lag_p
+            total = wide(gf_sum, span(k), x)
+            for d in range(1, n_x):
+                send_p(k, d).wait_recv()
+                total = total + wide(rx, d - 1, span(k))
+            out_first[span(k)] = total.astype(jnp.bfloat16)
+
+    def sent(ref, sem, count=chunks):
+        if count:
+            got = ref.at[pl.ds(0, count * group)]
+            pltpu.make_async_copy(got, got, sem).wait()
+
+    early = z_first_count(chunks)
     for d in range(1, n_col):
         sent(own, fs.at[d - 1])
     for d in range(1, n_z):
         sent(own, zs.at[d - 1])
     for d in range(1, ratio):
-        sent(v1, ys.at[d - 1])
-        sent(own, hs.at[d - 1])
+        sent(own, hy.at[d - 1])
+
+        @pl.when(jnp.logical_not(home))
+        def _():
+            sent(v1, ys.at[d - 1])
+
+        sent(own, hs.at[d - 1], early)
+        sent(turn_in.at[d - 1], us.at[d - 1], chunks - early)
     for d in range(1, n_x):
         sent(own, ps.at[d - 1])
     sent(rc, cs)
     for b in range(bits):
-        sent(halves[b], bs.at[b])
+        sent(halves[b], bs.at[b], early)
+        sent(thin_in[b], ts.at[b], chunks - early)
 
 
 def turn_kernel(first, second, out_first, out_second):
@@ -278,7 +359,7 @@
     dma = lambda *shape: pltpu.SemaphoreType.DMA(shape)
     first, second = pl.pallas_call(
         functools.partial(kernel, n_row, n_col, chunks, group),
-        out_shape=[jax.ShapeDtypeStruct((freqs, shard, width), bf)] * 2,
+        out_shape=[pltpu.VMEM((freqs, shard, width), bf)] * 2,
         in_specs=[
             pl.BlockSpec(memory_space=pl.ANY),
         ] * 5,
@@ -300,27 +381,30 @@
             [vm(freqs, n_z // 2 ** (b + 1), ratio, shard, width) for b in range(bits)],
             vm(freqs, ratio, shard, width),
             vm(ratio - 1, freqs, shard, width),
+            vm(ratio - 1, freqs, n_z // 2, 2, shard, width),
+            [vm(freqs, n_z // 2 ** (b + 1), 2, shard, width) for b in range(bits)],
+            [vm(freqs, n_z // 2 ** (b + 1), shard, width) for b in range(bits)],
             dma(5), pltpu.SemaphoreType.DMA,
             dma(n_col - 1), dma(chunks),
-            dma(n_z - 1), dma(chunks), dma(chunks),
+            dma(n_z - 1), dma(chunks), dma(chunks), dma(ratio - 1),
             dma(ratio - 1), dma(ratio - 1, chunks),
             pltpu.SemaphoreType.DMA, dma(chunks),
             dma(n_x - 1), dma(n_x - 1, chunks),
+            dma(ratio - 1), dma(ratio - 1, chunks),
+            dma(bits), dma(bits, chunks),
             dma(ratio - 1), dma(ratio - 1, chunks),
             dma(bits), dma(bits, chunks),
         ],
         compiler_params=pltpu.CompilerParams(collective_id=0, has_side_effects=True),
         name="adjoint",
     )(spectra, window_flags, pair_mask, misfit_weight, observed)
-    parts = 2 if shard % 32 == 0 else 1
     first, second = pl.pallas_call(
         turn_kernel,
         out_shape=[jax.ShapeDtypeStruct((shard, freqs, width), bf)] * 2,
-        grid=(parts,),
-        in_specs=[pl.BlockSpec((freqs, shard // parts, width), lambda i: (0, i, 0))] * 2,
-        out_specs=[pl.BlockSpec((shard // parts, freqs, width), lambda i: (i, 0, 0))] * 2,
+        in_specs=[pl.BlockSpec(memory_space=pltpu.VMEM)] * 2,
+        out_specs=[pl.BlockSpec(memory_space=pltpu.VMEM)] * 2,
         name="turn",
-    )(first, second)
+    )(*(pltpu.with_memory_space_constraint(part, pltpu.VMEM) for part in (first, second)))
     return first, second[None]
 
 

time: 40.6 us -> 37.4 us (0.921)
  Pallas kernels: 39.7 us -> 36.6 us
    pallas_call x1, Pallas kernels: 38.1 us -> 35.9 us  [per_device(): pl.pallas_call(functools.partial(kernel, n_row, n_col, chunks, group), ou...]
    pallas_call x1, Pallas kernels: 1.66 us -> 0.77 us  [per_device(): pl.pallas_call(turn_kernel, out_shape=[jax.ShapeDtypeStruct((shard, freqs...]
where the time goes in v1:
time: 37.4 us; the launch traced here: 37.3 us
  Pallas kernels  36.6 us (98%)
  between operations  0.64 us (2%)
    pallas_call x1, Pallas kernels, per_device(): pl.pallas_call(functools.partial(kernel, n_row, n_col, chunks, group), ou...  35.9 us
    pallas_call x1, Pallas kernels, per_device(): pl.pallas_call(turn_kernel, out_shape=[jax.ShapeDtypeStruct((shard, freqs...  0.77 us

profile of v1, /device:TPU:0, one launch (start us, length us, event | category | flops | bytes accessed | tf_op | source)
XLA Modules:
  0.0 37.3 jit_solution(14809187220790096091)
XLA Ops:
  0.6 35.9 %adjoint.1 = (bf16[16,32,128]{2,1,0:T(8,128)(2,1)S(1)}, bf16[16,32,128]{2,1,0:T(8,128)(2,1)S(1)}) custom-call(bf16[32,16,128]{2,1,0:T(8,128)(2,1)} %raw_hbm.1, s32[32,64]{1,0:T(8,128)} %flags_hbm.1, s32[128,256]{1,0:T(8,128)} %mask_hbm.1, bf16[16,128,256]{2,1,0:T(8,128)(2,1)} %w_hbm.1, bf16[2,16,128,256]{3,2,1,0:T(8,128)(2,1)} %obs_hbm.1), custom_call_target="tpu_custom_call" | custom-call | tf_op jit(solution)/shard_map/adjoint/pallas_call | solution.py:360
  36.5 0.8 %turn.1 = (bf16[32,16,128]{2,1,0:T(8,128)(2,1)}, bf16[32,16,128]{2,1,0:T(8,128)(2,1)}) custom-call(bf16[16,32,128]{2,1,0:T(8,128)(2,1)S(1)} %get-tuple-element.6.first, bf16[16,32,128]{2,1,0:T(8,128)(2,1)S(1)} %get-tuple-element.7.second), custom_call_target="tpu_custom_call" | custom-call | tf_op jit(solution)/shard_map/turn/pallas_call | solution.py:401

commit v2 on v1

--- a/solution.py
+++ b/solution.py
@@ -12,29 +12,37 @@
 LAG_Y = 3
 LAG_STAGES = (4, 4, 4)
 LAG_C, LAG_P = 3, 4
-Z_FIRST_FROM, Z_FIRST_TO = 0, 8
-
-
-def z_first(k, chunks):
-    return jnp.logical_and(k * 16 >= Z_FIRST_FROM * chunks, k * 16 < Z_FIRST_TO * chunks)
-
-
-def z_first_count(chunks):
-    return sum(Z_FIRST_FROM * chunks <= k * 16 < Z_FIRST_TO * chunks for k in range(chunks))
+Z_FIRST = (0, 1, 2, 3)
+STRAIGHT = (5, 6, 7)
+LAG_F = 0
+
+
+def among(k, some):
+    yes = k < 0
+    for one in some:
+        yes = jnp.logical_or(yes, k == one)
+    return yes
+
+
+def z_first(k):
+    return among(k, Z_FIRST)
+
+
+def straight(k):
+    return among(k, STRAIGHT)
 
 
 def kernel(
     n_row, n_col, chunks, group,
     raw_hbm, flags_hbm, mask_hbm, w_hbm, obs_hbm, out_first, out_second,
     raw, flags, mask, own,
-    v1, v2, w_v, obs_v, gf, gf_sum, rc, rx, sums, halves, last, ry, turn_in, thin, thin_in,
-    in_sem, own_sem, fs, fr, zs, zr, lz, hy, ys, yr,
-    cs, cr, ps, pr, hs, hr, bs, br, us, ur, ts, tr,
+    v1, v2, w_v, obs_v, gf, gf_sum, rc, rx, sums, got_wide, total_wide, box_wide, last, ry, turn_in, thin, got_thin, total_thin, box_thin, straight_in,
+    in_sem, own_sem, fx, xr, fs, fr, fn, zs, zr, lz, hy, ys, yr,
+    cs, cr, ps, pr, hs, hr, us, ur, zw, zt, mr, br, ds, dr,
 ):
     ratio = n_row // n_col
     n_z = n_row // ratio
     n_x = n_col // 2
-    bits = n_z.bit_length() - 1
     row, col = lax.axis_index("row"), lax.axis_index("col")
     z, y = row // ratio, row % ratio
     x, core = col // 2, col % 2
@@ -63,11 +71,19 @@
             device_id=(to_row, to_col), device_id_type=MESH,
         )
 
-    def send_f(k, d):
-        return remote(own.at[span(k)], v1.at[span(k), col], fs.at[d - 1], fr.at[k], row, (col + d) % n_col)
+    def send_x(k, d):
+        return remote(own.at[span(k)], v1.at[span(k), col], fx.at[d - 1], xr.at[k], row, col_at(d))
+
+    def send_own(k):
+        return remote(own.at[span(k)], v1.at[span(k), col], fs, fr.at[k], row, partner)
+
+    def send_on(k, d):
+        got = v1.at[span(k), col_at(d)]
+        return remote(got, got, fn.at[d - 1], fr.at[k], row, partner)
 
     def send_z(k, d):
-        return remote(own.at[span(k)], v2.at[span(k), y, col], zs.at[d - 1], zr.at[k], row_z(d), z)
+        to_z = jnp.where(d <= z, z - d, d)
+        return remote(own.at[span(k)], v2.at[span(k), y, col], zs.at[d - 1], zr.at[k], to_z * ratio + y, z)
 
     def send_home(k, d):
         return remote(own.at[span(k)], v2.at[span(k), y, col], hy.at[d - 1], yr.at[d - 1, k], row_y(d), z)
@@ -82,23 +98,26 @@
     def send_p(k, d):
         return remote(gf_sum.at[span(k), (x + d) % n_x], rx.at[d - 1, span(k)], ps.at[d - 1], pr.at[d - 1, k], row, col_at(d))
 
-    def bit(b):
-        return (z // 2**b) % 2
-
-    def row_bit(b):
-        return (z + (1 - 2 * bit(b)) * 2**b) * ratio + y
-
-    def send_b(k, b):
-        return remote(sums[b].at[span(k), :, 1 - bit(b)], halves[b].at[span(k)], bs.at[b], br.at[b, k], row_bit(b), col)
+    upper = (z // (n_z // 2)) % 2
+    outer = z % 2 == upper
+    mate = z + 1 - 2 * (z % 2)
+
+    def send_mate(k, d, src, dst, sem):
+        at = (z + d) % n_z
+        return remote(src.at[span(k), at], dst.at[span(k), at], sem, mr.at[k], mate * ratio + y, col)
+
+    def send_box(k, d, src, dst, sem):
+        at = (z + d) % n_z
+        return remote(src.at[span(k), at], dst.at[z // 2, span(k)], sem, br.at[k], row_z(d), col)
 
     def send_h(k, d):
         return remote(last.at[span(k), (y + d) % ratio], ry.at[d - 1, span(k)], hs.at[d - 1], hr.at[d - 1, k], row_y(d), col)
 
     def send_u(k, d):
-        return remote(sums[0].at[span(k), :, :, (y + d) % ratio], turn_in.at[d - 1, span(k)], us.at[d - 1], ur.at[d - 1, k], row_y(d), col)
-
-    def send_t(k, b):
-        return remote(thin[b].at[span(k), :, 1 - bit(b)], thin_in[b].at[span(k)], ts.at[b], tr.at[b, k], row_bit(b), col)
+        return remote(sums.at[span(k), :, (y + d) % ratio], turn_in.at[d - 1, span(k)], us.at[d - 1], ur.at[d - 1, k], row_y(d), col)
+
+    def send_s(k, d):
+        return remote(thin.at[span(k), (z + d) % n_z], straight_in.at[d - 1, span(k)], ds.at[d - 1], dr.at[k], row_z(d), col)
 
     home = z == col
 
@@ -127,8 +146,8 @@
             for j in range(n_col):
                 tell(row_y(d), j)
 
-    for b in range(bits):
-        tell(row_bit(b), col)
+    for d in range(1, n_z):
+        tell(row_z(d), col)
     for d in range(1, ratio):
         tell(row_y(d), col)
     for d in range(1, n_col):
@@ -144,21 +163,34 @@
     flagged = raw[...].astype(jnp.float32) * flag_both[:, None, :]
     own[...] = jnp.transpose(flagged, (1, 0, 2)).astype(jnp.bfloat16)
     load_own.start()
-    pl.semaphore_wait(barrier, n_col - 1 + n_z - 1 + bits + 2 * (ratio - 1))
+    pl.semaphore_wait(barrier, n_col - 1 + 2 * (n_z - 1) + 2 * (ratio - 1))
 
     @pl.loop(0, chunks)
     def _(k):
+        for d in range(1, n_x):
+            send_x(k, d).start()
         for d in range(n_z - 1, 0, -1):
-            send_z(k, d).start()
-        for d in range(1, n_col):
-            send_f(k, d).start()
+            @pl.when(d <= z)
+            def _():
+                send_z(k, d).start()
+        for d in range(n_z - 1, 0, -1):
+            @pl.when(d > z)
+            def _():
+                send_z(k, d).start()
         for d in range(1, ratio):
             send_home(k, d).start()
+        send_own(k).start()
 
     load_own.wait()
 
+    def pass_first(k):
+        got = v1.at[span(k), pl.ds(0, n_x - 1)]
+        pltpu.make_async_copy(got, got, xr.at[k]).wait()
+        for d in range(1, n_x):
+            send_on(k, d).start()
+
     def wait_first(k):
-        got = v1.at[span(k), pl.ds(0, n_col - 1)]
+        got = v1.at[span(k), pl.ds(0, n_x)]
         pltpu.make_async_copy(got, got, fr.at[k]).wait()
 
     def local_copy(k):
@@ -185,59 +217,117 @@
         g1 = t[:first_rows] - pltpu.roll(t[first_rows:], half, 1) * low_plus
         gf[f] = g1.reshape(n_x, 2, shard, 2 * half).astype(jnp.bfloat16)
         g2 = lax.dot_general(res, w, (((0,), (0,)), ((), ())), preferred_element_type=jnp.float32)
-        sums[0][f] = g2.reshape(n_z // 2, 2, ratio, shard, 2 * half).astype(jnp.bfloat16)
+        sums[f] = g2.reshape(n_z, ratio, shard, 2 * half).astype(jnp.bfloat16)
 
     def wide(ref, *at):
         return ref[at].astype(jnp.float32)
 
+    def to_mate(k, src, dst, sem):
+        @pl.when(outer)
+        def _():
+            for d in range(1, n_z):
+                send_mate(k, d, src, dst, sem).start()
+
+    def fold(k, src, got, total, box, sem):
+        @pl.when(jnp.logical_not(outer))
+        def _():
+            all_of = got.at[span(k), pl.ds(0, n_z - 1)]
+            pltpu.make_async_copy(all_of, all_of, mr.at[k]).wait()
+            total[span(k), mate] = src[span(k), mate]
+            for d in range(1, n_z):
+                at = (mate + d) % n_z
+                total[span(k), at] = (wide(src, span(k), at) + wide(got, span(k), at)).astype(jnp.bfloat16)
+            for d in range(1, n_z):
+                send_box(k, d, total, box, sem).start()
+
+    def unfold(k, src, total, box, put):
+        pairs = n_z // 2
+
+        def boxes(count):
+            all_of = box.at[pl.ds(0, count), span(k)]
+            pltpu.make_async_copy(all_of, all_of, br.at[k]).wait()
+
+        @pl.when(outer)
+        def _():
+            boxes(pairs)
+            out = wide(src, span(k), z)
+            for m in range(pairs):
+                out = out + wide(box, m, span(k))
+            put(out.astype(jnp.bfloat16))
+
+        @pl.when(jnp.logical_not(outer))
+        def _():
+            if pairs > 1:
+                boxes(pairs - 1)
+            out = wide(total, span(k), z)
+            for m in range(1, pairs):
+                out = out + wide(box, (z // 2 + m) % pairs, span(k))
+            put(out.astype(jnp.bfloat16))
+
     def second_stage(k, step):
-        if step < bits:
-            @pl.when(z_first(k, chunks))
-            def _():
-                send_b(k, step).wait_recv()
-                total = wide(sums[step], span(k), slice(None), bit(step)) + wide(halves[step], span(k))
-                if step + 1 < bits:
-                    sums[step + 1][span(k)] = total.reshape(
-                        group, n_z // 2 ** (step + 2), 2, ratio, shard, 2 * half
-                    ).astype(jnp.bfloat16)
-                    send_b(k, step + 1).start()
-                else:
-                    last[span(k)] = total[:, 0].astype(jnp.bfloat16)
-                    for d in range(1, ratio):
-                        send_h(k, d).start()
-        else:
-            @pl.when(z_first(k, chunks))
-            def _():
+        plain = jnp.logical_not(jnp.logical_or(z_first(k), straight(k)))
+
+        def put_last(value):
+            last[span(k)] = value
+            for d in range(1, ratio):
+                send_h(k, d).start()
+
+        def put_out(value):
+            out_second[span(k)] = value
+
+        @pl.when(z_first(k))
+        def _():
+            if step == 0:
+                fold(k, sums, got_wide, total_wide, box_wide, zw)
+            elif step == 1:
+                unfold(k, sums, total_wide, box_wide, put_last)
+            else:
                 total = wide(last, span(k), y)
                 for d in range(1, ratio):
                     send_h(k, d).wait_recv()
                     total = total + wide(ry, d - 1, span(k))
-                out_second[span(k)] = total.astype(jnp.bfloat16)
-
-        @pl.when(jnp.logical_not(z_first(k, chunks)))
-        def _():
-            if step == 0:
-                total = wide(sums[0], span(k), slice(None), slice(None), y)
+                put_out(total.astype(jnp.bfloat16))
+
+        if step == 0:
+            @pl.when(jnp.logical_not(z_first(k)))
+            def _():
+                total = wide(sums, span(k), slice(None), y)
                 for d in range(1, ratio):
                     send_u(k, d).wait_recv()
                     total = total + wide(turn_in, d - 1, span(k))
-            else:
-                b = step - 1
-                send_t(k, b).wait_recv()
-                total = wide(thin[b], span(k), slice(None), bit(b)) + wide(thin_in[b], span(k))
-            if step < bits:
-                thin[step][span(k)] = total.reshape(
-                    group, n_z // 2 ** (step + 1), 2, shard, 2 * half
-                ).astype(jnp.bfloat16)
-                send_t(k, step).start()
-            else:
-                out_second[span(k)] = total[:, 0].astype(jnp.bfloat16)
+                thin[span(k)] = total.astype(jnp.bfloat16)
+
+                @pl.when(straight(k))
+                def _():
+                    for d in range(1, n_z):
+                        send_s(k, d).start()
+
+                @pl.when(jnp.logical_not(straight(k)))
+                def _():
+                    to_mate(k, thin, got_thin, zt)
+        else:
+            @pl.when(plain)
+            def _():
+                if step == 1:
+                    fold(k, thin, got_thin, total_thin, box_thin, zt)
+                else:
+                    unfold(k, thin, total_thin, box_thin, put_out)
+
+        if step == 1:
+            @pl.when(straight(k))
+            def _():
+                got = straight_in.at[:, span(k)]
+                pltpu.make_async_copy(got, got, dr.at[k]).wait()
+                total = wide(thin, span(k), z)
+                for d in range(1, n_z):
+                    total = total + wide(straight_in, d - 1, span(k))
+                put_out(total.astype(jnp.bfloat16))
 
     lag_y = LAG_Y
     lag_c = lag_y + LAG_C
     lag_p = lag_c + LAG_P
     lag_s, at = [], lag_y
-    for step in range(bits + 1):
+    for step in range(3):
         at = at + LAG_STAGES[min(step, len(LAG_STAGES) - 1)]
         lag_s.append(at)
 
@@ -245,11 +335,6 @@
     def _(it):
         @pl.when(it < chunks)
         def _():
-            @pl.when(home)
-            def _():
-                wait_first(it)
-                local_copy(it).start()
-
             @pl.when(jnp.logical_not(home))
             def _():
                 got = v2.at[span(it), y]
@@ -257,6 +342,10 @@
                 for d in range(1, ratio):
                     send_y(it, d).start()
 
+        @pl.when(jnp.logical_and(it >= LAG_F, it < chunks + LAG_F))
+        def _():
+            pass_first(it - LAG_F)
+
         @pl.when(jnp.logical_and(it >= lag_y, it < chunks + lag_y))
         def _():
             k = it - lag_y
@@ -270,29 +359,28 @@
             for d in range(1, ratio):
                 send_y(k, d).wait_recv()
 
+            wait_first(k)
+
             @pl.when(home)
             def _():
+                local_copy(k).start()
                 local_copy(k).wait()
-
-            @pl.when(jnp.logical_not(home))
-            def _():
-                wait_first(k)
 
             for i in range(group):
                 compute(k * group + i)
 
-            @pl.when(z_first(k, chunks))
-            def _():
-                send_b(k, 0).start()
-
-            @pl.when(jnp.logical_not(z_first(k, chunks)))
+            @pl.when(z_first(k))
+            def _():
+                to_mate(k, sums, got_wide, zw)
+
+            @pl.when(jnp.logical_not(z_first(k)))
             def _():
                 for d in range(1, ratio):
                     send_u(k, d).start()
 
             send_c(k).start()
 
-        for step in range(bits + 1):
+        for step in range(3):
             @pl.when(jnp.logical_and(it >= lag_s[step], it < chunks + lag_s[step]))
             def _():
                 second_stage(it - lag_s[step], step)
@@ -320,9 +408,14 @@
             got = ref.at[pl.ds(0, count * group)]
             pltpu.make_async_copy(got, got, sem).wait()
 
-    early = z_first_count(chunks)
-    for d in range(1, n_col):
-        sent(own, fs.at[d - 1])
+    early = sum(k in Z_FIRST for k in range(chunks))
+    last_ones = sum(k in STRAIGHT for k in range(chunks))
+    for d in range(1, n_z):
+        sent(own, ds.at[d - 1], last_ones)
+    sent(own, fs)
+    for d in range(1, n_x):
+        sent(own, fx.at[d - 1])
+        sent(own, fn.at[d - 1])
     for d in range(1, n_z):
         sent(own, zs.at[d - 1])
     for d in range(1, ratio):
@@ -337,9 +430,8 @@
     for d in range(1, n_x):
         sent(own, ps.at[d - 1])
     sent(rc, cs)
-    for b in range(bits):
-        sent(halves[b], bs.at[b], early)
-        sent(thin_in[b], ts.at[b], chunks - early)
+    sent(got_wide.at[:, pl.ds(0, n_z - 1)], zw, early)
+    sent(got_thin.at[:, pl.ds(0, n_z - 1)], zt, chunks - early - last_ones)
 
 
 def turn_kernel(first, second, out_first, out_second):
@@ -351,7 +443,6 @@
     shard, freqs, width = spectra.shape
     ratio = n_row // n_col
     n_z, n_x = n_row // ratio, n_col // 2
-    bits = n_z.bit_length() - 1
     group = GROUP if freqs % GROUP == 0 else 1
     chunks = freqs // group
     bf = jnp.bfloat16
@@ -377,23 +468,28 @@
             vm(freqs, n_x, shard, width),
             vm(freqs, n_x, shard, width),
             vm(n_x - 1, freqs, shard, width),
-            [vm(freqs, n_z // 2 ** (b + 1), 2, ratio, shard, width) for b in range(bits)],
-            [vm(freqs, n_z // 2 ** (b + 1), ratio, shard, width) for b in range(bits)],
+            vm(freqs, n_z, ratio, shard, width),
+            vm(freqs, n_z, ratio, shard, width),
+            vm(freqs, n_z, ratio, shard, width),
+            vm(n_z // 2, freqs, ratio, shard, width),
             vm(freqs, ratio, shard, width),
             vm(ratio - 1, freqs, shard, width),
-            vm(ratio - 1, freqs, n_z // 2, 2, shard, width),
-            [vm(freqs, n_z // 2 ** (b + 1), 2, shard, width) for b in range(bits)],
-            [vm(freqs, n_z // 2 ** (b + 1), shard, width) for b in range(bits)],
+            vm(ratio - 1, freqs, n_z, shard, width),
+            vm(freqs, n_z, shard, width),
+            vm(freqs, n_z, shard, width),
+            vm(freqs, n_z, shard, width),
+            vm(n_z // 2, freqs, shard, width),
+            vm(n_z - 1, freqs, shard, width),
             dma(5), pltpu.SemaphoreType.DMA,
-            dma(n_col - 1), dma(chunks),
+            dma(n_x - 1), dma(chunks), pltpu.SemaphoreType.DMA, dma(chunks), dma(n_x - 1),
             dma(n_z - 1), dma(chunks), dma(chunks), dma(ratio - 1),
             dma(ratio - 1), dma(ratio - 1, chunks),
             pltpu.SemaphoreType.DMA, dma(chunks),
             dma(n_x - 1), dma(n_x - 1, chunks),
             dma(ratio - 1), dma(ratio - 1, chunks),
-            dma(bits), dma(bits, chunks),
             dma(ratio - 1), dma(ratio - 1, chunks),
-            dma(bits), dma(bits, chunks),
+            pltpu.SemaphoreType.DMA, pltpu.SemaphoreType.DMA, dma(chunks), dma(chunks),
+            dma(n_z - 1), dma(chunks),
         ],
         compiler_params=pltpu.CompilerParams(collective_id=0, has_side_effects=True),
         name="adjoint",

time: 37.4 us -> 36.1 us (0.965)
  Pallas kernels: 36.6 us -> 35.2 us
    pallas_call x1, Pallas kernels: 35.9 us -> 34.5 us  [per_device(): pl.pallas_call(functools.partial(kernel, n_row, n_col, chunks, group), ou...]
where the time goes in v2:
time: 36.1 us; the launch traced here: 35.9 us
  Pallas kernels  35.2 us (98%)
  between operations  0.64 us (2%)
    pallas_call x1, Pallas kernels, per_device(): pl.pallas_call(functools.partial(kernel, n_row, n_col, chunks, group), ou...  34.5 us
    pallas_call x1, Pallas kernels, per_device(): pl.pallas_call(turn_kernel, out_shape=[jax.ShapeDtypeStruct((shard, freqs...  0.77 us

profile of v2, /device:TPU:0, one launch (start us, length us, event | category | flops | bytes accessed | tf_op | source)
XLA Modules:
  0.0 35.9 jit_solution(678514668243073204)
XLA Ops:
  0.6 34.5 %adjoint.1 = (bf16[16,32,128]{2,1,0:T(8,128)(2,1)S(1)}, bf16[16,32,128]{2,1,0:T(8,128)(2,1)S(1)}) custom-call(bf16[32,16,128]{2,1,0:T(8,128)(2,1)} %raw_hbm.1, s32[32,64]{1,0:T(8,128)} %flags_hbm.1, s32[128,256]{1,0:T(8,128)} %mask_hbm.1, bf16[16,128,256]{2,1,0:T(8,128)(2,1)} %w_hbm.1, bf16[2,16,128,256]{3,2,1,0:T(8,128)(2,1)} %obs_hbm.1), custom_call_target="tpu_custom_call" | custom-call | tf_op jit(solution)/shard_map/adjoint/pallas_call | solution.py:451
  35.1 0.8 %turn.1 = (bf16[32,16,128]{2,1,0:T(8,128)(2,1)}, bf16[32,16,128]{2,1,0:T(8,128)(2,1)}) custom-call(bf16[16,32,128]{2,1,0:T(8,128)(2,1)S(1)} %get-tuple-element.6.first, bf16[16,32,128]{2,1,0:T(8,128)(2,1)S(1)} %get-tuple-element.7.second), custom_call_target="tpu_custom_call" | custom-call | tf_op jit(solution)/shard_map/turn/pallas_call | solution.py:497

commit v3 on v2

--- a/solution.py
+++ b/solution.py
@@ -15,6 +15,7 @@
 Z_FIRST = (0, 1, 2, 3)
 STRAIGHT = (5, 6, 7)
 LAG_F = 0
+BLOCK = 4
 
 
 def among(k, some):
@@ -37,8 +38,8 @@
     raw_hbm, flags_hbm, mask_hbm, w_hbm, obs_hbm, out_first, out_second,
     raw, flags, mask, own,
     v1, v2, w_v, obs_v, gf, gf_sum, rc, rx, sums, got_wide, total_wide, box_wide, last, ry, turn_in, thin, got_thin, total_thin, box_thin, straight_in,
-    in_sem, own_sem, fx, xr, fs, fr, fn, zs, zr, lz, hy, ys, yr,
-    cs, cr, ps, pr, hs, hr, us, ur, zw, zt, mr, br, ds, dr,
+    in_sem, own_sem, xr, fs, fr, zs, zr, lz, hy, ys, yr,
+    cs, cr, ps, pr, hs, us, ur, zw, zt, mr, br, ds,
 ):
     ratio = n_row // n_col
     n_z = n_row // ratio
@@ -62,6 +63,11 @@
     def row_z(step):
         return ((z + step) % n_z) * ratio + y
 
+    block = BLOCK if chunks % BLOCK == 0 else 1
+
+    def wide_span(b):
+        return pl.ds(b * block * group, block * group)
+
     def span(k):
         return pl.ds(k * group, group)
 
@@ -72,18 +78,18 @@
         )
 
     def send_x(k, d):
-        return remote(own.at[span(k)], v1.at[span(k), col], fx.at[d - 1], xr.at[k], row, col_at(d))
+        return remote(own.at[span(k)], v1.at[span(k), col], fs, xr.at[k], row, col_at(d))
 
     def send_own(k):
         return remote(own.at[span(k)], v1.at[span(k), col], fs, fr.at[k], row, partner)
 
     def send_on(k, d):
         got = v1.at[span(k), col_at(d)]
-        return remote(got, got, fn.at[d - 1], fr.at[k], row, partner)
+        return remote(got, got, fs, fr.at[k], row, partner)
 
     def send_z(k, d):
         to_z = jnp.where(d <= z, z - d, d)
-        return remote(own.at[span(k)], v2.at[span(k), y, col], zs.at[d - 1], zr.at[k], to_z * ratio + y, z)
+        return remote(own.at[span(k)], v2.at[span(k), y, col], zs, zr.at[k], to_z * ratio + y, z)
 
     def send_home(k, d):
         return remote(own.at[span(k)], v2.at[span(k), y, col], hy.at[d - 1], yr.at[d - 1, k], row_y(d), z)
@@ -93,10 +99,11 @@
         return remote(src, src, ys.at[d - 1], yr.at[d - 1, k], row_y(d), col)
 
     def send_c(k):
-        return remote(gf.at[span(k), :, 1 - core], rc.at[span(k)], cs, cr.at[k], row, partner)
-
-    def send_p(k, d):
-        return remote(gf_sum.at[span(k), (x + d) % n_x], rx.at[d - 1, span(k)], ps.at[d - 1], pr.at[d - 1, k], row, col_at(d))
+        return remote(gf.at[span(k), :, 1 - core], rc.at[span(k)], cs, cr.at[k // block], row, partner)
+
+    def send_p(b, d):
+        at = wide_span(b)
+        return remote(gf_sum.at[at, (x + d) % n_x], rx.at[d - 1, at], ps.at[d - 1], pr.at[d - 1, b], row, col_at(d))
 
     upper = (z // (n_z // 2)) % 2
     outer = z % 2 == upper
@@ -111,13 +118,13 @@
         return remote(src.at[span(k), at], dst.at[z // 2, span(k)], sem, br.at[k], row_z(d), col)
 
     def send_h(k, d):
-        return remote(last.at[span(k), (y + d) % ratio], ry.at[d - 1, span(k)], hs.at[d - 1], hr.at[d - 1, k], row_y(d), col)
+        return remote(last.at[span(k), (y + d) % ratio], ry.at[d - 1, span(k)], hs.at[d - 1], ur.at[d - 1, k], row_y(d), col)
 
     def send_u(k, d):
         return remote(sums.at[span(k), :, (y + d) % ratio], turn_in.at[d - 1, span(k)], us.at[d - 1], ur.at[d - 1, k], row_y(d), col)
 
     def send_s(k, d):
-        return remote(thin.at[span(k), (z + d) % n_z], straight_in.at[d - 1, span(k)], ds.at[d - 1], dr.at[k], row_z(d), col)
+        return remote(thin.at[span(k), (z + d) % n_z], straight_in.at[d - 1, span(k)], ds, br.at[k], row_z(d), col)
 
     home = z == col
 
@@ -194,7 +201,7 @@
         pltpu.make_async_copy(got, got, fr.at[k]).wait()
 
     def local_copy(k):
-        return pltpu.make_async_copy(v1.at[span(k)], v2.at[span(k), y], lz.at[k])
+        return pltpu.make_async_copy(v1.at[span(k)], v2.at[span(k), y], lz)
 
     lane = lax.broadcasted_iota(jnp.int32, (1, 2 * half), 1)
     low_plus = jnp.where(lane < half, 1.0, -1.0).astype(jnp.float32)
@@ -317,7 +324,7 @@
             @pl.when(straight(k))
             def _():
                 got = straight_in.at[:, span(k)]
-                pltpu.make_async_copy(got, got, dr.at[k]).wait()
+                pltpu.make_async_copy(got, got, br.at[k]).wait()
                 total = wide(thin, span(k), z)
                 for d in range(1, n_z):
                     total = total + wide(straight_in, d - 1, span(k))
@@ -331,8 +338,44 @@
         at = at + LAG_STAGES[min(step, len(LAG_STAGES) - 1)]
         lag_s.append(at)
 
+    def sent(ref, sem, count=chunks):
+        if count:
+            got = ref.at[pl.ds(0, count * group)]
+            pltpu.make_async_copy(got, got, sem).wait()
+
+    early = sum(k in Z_FIRST for k in range(chunks))
+    last_ones = sum(k in STRAIGHT for k in range(chunks))
+
+    def gather_sent():
+        sent(v1.at[:, pl.ds(0, n_col - 1)], fs)
+        pltpu.make_async_copy(straight_in, straight_in, zs).wait()
+        for d in range(1, ratio):
+            sent(own, hy.at[d - 1])
+
+            @pl.when(jnp.logical_not(home))
+            def _():
+                sent(v1, ys.at[d - 1])
+
+    def sums_sent():
+        sent(rc, cs)
+        sent(got_wide.at[:, pl.ds(0, n_z - 1)], zw, early)
+        for d in range(1, ratio):
+            sent(own, hs.at[d - 1], early)
+            sent(turn_in.at[d - 1], us.at[d - 1], chunks - early)
+
+    last_wide = max([k for k in range(chunks) if k in Z_FIRST], default=0)
+    sums_done = max(chunks + lag_c, last_wide + lag_s[1] + 1)
+
     @pl.loop(0, chunks + max(lag_s[-1], lag_p))
     def _(it):
+        @pl.when(it == chunks + lag_y + 1)
+        def _():
+            gather_sent()
+
+        @pl.when(it == sums_done + 1)
+        def _():
+            sums_sent()
+
         @pl.when(it < chunks)
         def _():
             @pl.when(jnp.logical_not(home))
@@ -385,53 +428,35 @@
             def _():
                 second_stage(it - lag_s[step], step)
 
-        @pl.when(jnp.logical_and(it >= lag_c, it < chunks + lag_c))
-        def _():
-            k = it - lag_c
-            send_c(k).wait_recv()
-            total = wide(gf, span(k), slice(None), core) + wide(rc, span(k))
-            gf_sum[span(k)] = total.astype(jnp.bfloat16)
+        def full_block(lag):
+            return jnp.logical_and(jnp.logical_and(it >= lag, it < chunks + lag), (it - lag) % block == block - 1)
+
+        @pl.when(full_block(lag_c))
+        def _():
+            b = (it - lag_c) // block
+            at = wide_span(b)
+            got = rc.at[at]
+            pltpu.make_async_copy(got, got, cr.at[b]).wait()
+            gf_sum[at] = (wide(gf, at, slice(None), core) + wide(rc, at)).astype(jnp.bfloat16)
             for d in range(1, n_x):
-                send_p(k, d).start()
-
-        @pl.when(jnp.logical_and(it >= lag_p, it < chunks + lag_p))
-        def _():
-            k = it - lag_p
-            total = wide(gf_sum, span(k), x)
+                send_p(b, d).start()
+
+        @pl.when(full_block(lag_p))
+        def _():
+            b = (it - lag_p) // block
+            at = wide_span(b)
+            total = wide(gf_sum, at, x)
             for d in range(1, n_x):
-                send_p(k, d).wait_recv()
-                total = total + wide(rx, d - 1, span(k))
-            out_first[span(k)] = total.astype(jnp.bfloat16)
-
-    def sent(ref, sem, count=chunks):
-        if count:
-            got = ref.at[pl.ds(0, count * group)]
-            pltpu.make_async_copy(got, got, sem).wait()
-
-    early = sum(k in Z_FIRST for k in range(chunks))
-    last_ones = sum(k in STRAIGHT for k in range(chunks))
-    for d in range(1, n_z):
-        sent(own, ds.at[d - 1], last_ones)
-    sent(own, fs)
-    for d in range(1, n_x):
-        sent(own, fx.at[d - 1])
-        sent(own, fn.at[d - 1])
-    for d in range(1, n_z):
-        sent(own, zs.at[d - 1])
-    for d in range(1, ratio):
-        sent(own, hy.at[d - 1])
-
-        @pl.when(jnp.logical_not(home))
-        def _():
-            sent(v1, ys.at[d - 1])
-
-        sent(own, hs.at[d - 1], early)
-        sent(turn_in.at[d - 1], us.at[d - 1], chunks - early)
+                send_p(b, d).wait_recv()
+                total = total + wide(rx, d - 1, at)
+            out_first[at] = total.astype(jnp.bfloat16)
+
+    sent(got_thin.at[:, pl.ds(0, n_z - 1)], zt, chunks - early - last_ones)
+    if last_ones:
+        all_of = straight_in.at[:, pl.ds(0, last_ones * group)]
+        pltpu.make_async_copy(all_of, all_of, ds).wait()
     for d in range(1, n_x):
         sent(own, ps.at[d - 1])
-    sent(rc, cs)
-    sent(got_wide.at[:, pl.ds(0, n_z - 1)], zw, early)
-    sent(got_thin.at[:, pl.ds(0, n_z - 1)], zt, chunks - early - last_ones)
 
 
 def turn_kernel(first, second, out_first, out_second):
@@ -448,6 +473,8 @@
     bf = jnp.bfloat16
     vm = lambda *shape: pltpu.VMEM(shape, bf)
     dma = lambda *shape: pltpu.SemaphoreType.DMA(shape)
+    one = pltpu.SemaphoreType.DMA
+    blocks = chunks // BLOCK if chunks % BLOCK == 0 else chunks
     first, second = pl.pallas_call(
         functools.partial(kernel, n_row, n_col, chunks, group),
         out_shape=[pltpu.VMEM((freqs, shard, width), bf)] * 2,
@@ -481,15 +508,12 @@
             vm(n_z // 2, freqs, shard, width),
             vm(n_z - 1, freqs, shard, width),
             dma(5), pltpu.SemaphoreType.DMA,
-            dma(n_x - 1), dma(chunks), pltpu.SemaphoreType.DMA, dma(chunks), dma(n_x - 1),
-            dma(n_z - 1), dma(chunks), dma(chunks), dma(ratio - 1),
+            dma(chunks), one, dma(chunks),
+            one, dma(chunks), one, dma(ratio - 1),
             dma(ratio - 1), dma(ratio - 1, chunks),
-            pltpu.SemaphoreType.DMA, dma(chunks),
-            dma(n_x - 1), dma(n_x - 1, chunks),
-            dma(ratio - 1), dma(ratio - 1, chunks),
-            dma(ratio - 1), dma(ratio - 1, chunks),
-            pltpu.SemaphoreType.DMA, pltpu.SemaphoreType.DMA, dma(chunks), dma(chunks),
-            dma(n_z - 1), dma(chunks),
+            one, dma(blocks), dma(n_x - 1), dma(n_x - 1, blocks),
+            dma(ratio - 1), dma(ratio - 1), dma(ratio - 1, chunks),
+            one, one, dma(chunks), dma(chunks), one,
         ],
         compiler_params=pltpu.CompilerParams(collective_id=0, has_side_effects=True),
         name="adjoint",

time: 36.1 us -> 35.8 us (level)
  no operation moved by 1% of the time
where the time goes in v3:
time: 35.8 us; the launch traced here: 35.5 us
  Pallas kernels  34.9 us (97%)
  between operations  0.64 us (2%)
    pallas_call x1, Pallas kernels, per_device(): pl.pallas_call(functools.partial(kernel, n_row, n_col, chunks, group), ou...  34.1 us
    pallas_call x1, Pallas kernels, per_device(): pl.pallas_call(turn_kernel, out_shape=[jax.ShapeDtypeStruct((shard, freqs...  0.77 us

profile of v3, /device:TPU:0, one launch (start us, length us, event | category | flops | bytes accessed | tf_op | source)
XLA Modules:
  0.0 35.5 jit_solution(3281119227518590792)
XLA Ops:
  0.6 34.1 %adjoint.1 = (bf16[16,32,128]{2,1,0:T(8,128)(2,1)S(1)}, bf16[16,32,128]{2,1,0:T(8,128)(2,1)S(1)}) custom-call(bf16[32,16,128]{2,1,0:T(8,128)(2,1)} %raw_hbm.1, s32[32,64]{1,0:T(8,128)} %flags_hbm.1, s32[128,256]{1,0:T(8,128)} %mask_hbm.1, bf16[16,128,256]{2,1,0:T(8,128)(2,1)} %w_hbm.1, bf16[2,16,128,256]{3,2,1,0:T(8,128)(2,1)} %obs_hbm.1), custom_call_target="tpu_custom_call" | custom-call | tf_op jit(solution)/shard_map/adjoint/pallas_call | solution.py:478
  34.7 0.8 %turn.1 = (bf16[32,16,128]{2,1,0:T(8,128)(2,1)}, bf16[32,16,128]{2,1,0:T(8,128)(2,1)}) custom-call(bf16[16,32,128]{2,1,0:T(8,128)(2,1)S(1)} %get-tuple-element.6.first, bf16[16,32,128]{2,1,0:T(8,128)(2,1)S(1)} %get-tuple-element.7.second), custom_call_target="tpu_custom_call" | custom-call | tf_op jit(solution)/shard_map/turn/pallas_call | solution.py:521

commit v4 on v3

--- a/solution.py
+++ b/solution.py
@@ -9,11 +9,11 @@
 
 MESH = pl.DeviceIdType.MESH
 GROUP = 2
-LAG_Y = 3
+LAG_Y = 4
 LAG_STAGES = (4, 4, 4)
 LAG_C, LAG_P = 3, 4
 Z_FIRST = (0, 1, 2, 3)
-STRAIGHT = (5, 6, 7)
+STRAIGHT = (6, 7)
 LAG_F = 0
 BLOCK = 4
 

time: 35.8 us -> 35.6 us (level)
  no operation moved by 1% of the time
where the time goes in v4:
time: 35.6 us; the launch traced here: 35.2 us
  Pallas kernels  34.6 us (97%)
  between operations  0.64 us (2%)
    pallas_call x1, Pallas kernels, per_device(): pl.pallas_call(functools.partial(kernel, n_row, n_col, chunks, group), ou...  33.8 us
    pallas_call x1, Pallas kernels, per_device(): pl.pallas_call(turn_kernel, out_shape=[jax.ShapeDtypeStruct((shard, freqs...  0.77 us

profile of v4, /device:TPU:0, one launch (start us, length us, event | category | flops | bytes accessed | tf_op | source)
XLA Modules:
  0.0 35.2 jit_solution(13959387701780233979)
XLA Ops:
  0.6 33.8 %adjoint.1 = (bf16[16,32,128]{2,1,0:T(8,128)(2,1)S(1)}, bf16[16,32,128]{2,1,0:T(8,128)(2,1)S(1)}) custom-call(bf16[32,16,128]{2,1,0:T(8,128)(2,1)} %raw_hbm.1, s32[32,64]{1,0:T(8,128)} %flags_hbm.1, s32[128,256]{1,0:T(8,128)} %mask_hbm.1, bf16[16,128,256]{2,1,0:T(8,128)(2,1)} %w_hbm.1, bf16[2,16,128,256]{3,2,1,0:T(8,128)(2,1)} %obs_hbm.1), custom_call_target="tpu_custom_call" | custom-call | tf_op jit(solution)/shard_map/adjoint/pallas_call | solution.py:478
  34.4 0.8 %turn.1 = (bf16[32,16,128]{2,1,0:T(8,128)(2,1)}, bf16[32,16,128]{2,1,0:T(8,128)(2,1)}) custom-call(bf16[16,32,128]{2,1,0:T(8,128)(2,1)S(1)} %get-tuple-element.6.first, bf16[16,32,128]{2,1,0:T(8,128)(2,1)S(1)} %get-tuple-element.7.second), custom_call_target="tpu_custom_call" | custom-call | tf_op jit(solution)/shard_map/turn/pallas_call | solution.py:521

commit v5 on v4

--- a/solution.py
+++ b/solution.py
@@ -11,11 +11,11 @@
 GROUP = 2
 LAG_Y = 4
 LAG_STAGES = (4, 4, 4)
-LAG_C, LAG_P = 3, 4
+LAG_C, LAG_P = 3, 5
 Z_FIRST = (0, 1, 2, 3)
 STRAIGHT = (6, 7)
 LAG_F = 0
-BLOCK = 4
+BLOCK = 8
 
 
 def among(k, some):

time: 35.6 us -> 35.6 us (level)
  no operation moved by 1% of the time
where the time goes in v5:
time: 35.6 us; the launch traced here: 35.2 us
  Pallas kernels  34.5 us (97%)
  between operations  0.64 us (2%)
    pallas_call x1, Pallas kernels, per_device(): pl.pallas_call(functools.partial(kernel, n_row, n_col, chunks, group), ou...  33.8 us
    pallas_call x1, Pallas kernels, per_device(): pl.pallas_call(turn_kernel, out_shape=[jax.ShapeDtypeStruct((shard, freqs...  0.77 us

profile of v5, /device:TPU:0, one launch (start us, length us, event | category | flops | bytes accessed | tf_op | source)
XLA Modules:
  0.0 35.2 jit_solution(9981538294124832908)
XLA Ops:
  0.6 33.8 %adjoint.1 = (bf16[16,32,128]{2,1,0:T(8,128)(2,1)S(1)}, bf16[16,32,128]{2,1,0:T(8,128)(2,1)S(1)}) custom-call(bf16[32,16,128]{2,1,0:T(8,128)(2,1)} %raw_hbm.1, s32[32,64]{1,0:T(8,128)} %flags_hbm.1, s32[128,256]{1,0:T(8,128)} %mask_hbm.1, bf16[16,128,256]{2,1,0:T(8,128)(2,1)} %w_hbm.1, bf16[2,16,128,256]{3,2,1,0:T(8,128)(2,1)} %obs_hbm.1), custom_call_target="tpu_custom_call" | custom-call | tf_op jit(solution)/shard_map/adjoint/pallas_call | solution.py:478
  34.4 0.8 %turn.1 = (bf16[32,16,128]{2,1,0:T(8,128)(2,1)}, bf16[32,16,128]{2,1,0:T(8,128)(2,1)}) custom-call(bf16[16,32,128]{2,1,0:T(8,128)(2,1)S(1)} %get-tuple-element.6.first, bf16[16,32,128]{2,1,0:T(8,128)(2,1)S(1)} %get-tuple-element.7.second), custom_call_target="tpu_custom_call" | custom-call | tf_op jit(solution)/shard_map/turn/pallas_call | solution.py:521
